TPU v7x, 32 devices: a whole 2x2x4 slice. The times are simulated.
32 devices in a mesh: wide: 8 (over z, x), narrow: 4 (over y, core).
Axes of the slice: x: 2, y: 2, z: 4, core: 2. Of those that a mesh axis runs over, the one named last changes fastest.
Arguments:
- positions: float32 [3, 4096], P(None, ('wide', 'narrow')), may hold values from -1 to 69, as said below
- noise: float32 [3, 16, 4096], P(None, None, ('wide', 'narrow')), may hold values from -6 to 6
Outputs:
- displacement: float32 [3, 16, 4096], P(None, None, ('wide', 'narrow'))
Inputs may be any that keep to these rules, and one draw needn't show every extreme that they name: `positions`: any two particles lie at least 1.2 apart.
All inputs are finite; a program needn't handle non-finite values.
Results may differ from a plain program's by a relative error of at most 0.0003.
Values sent between devices are 32-bit elements; how exact they have to be, the bound alone decides.
A program may use at most 64 MiB of HBM per device.

v0:
```python
import math
import jax
import jax.numpy as jnp
from jax import lax
from jax.sharding import PartitionSpec as P

ITERS = 3
ROOT_STEPS = 30
highest = lax.Precision.HIGHEST


def tile_factors(dist_sq, itself):
    safe_sq = jnp.where(itself, 4.0, dist_sq)
    radial = jnp.sqrt(safe_sq)
    inverse = 1.0 / radial
    far_scalar = 0.75 * inverse + 0.5 * inverse * inverse * inverse
    far_outer = (0.75 * inverse - 1.5 * inverse * inverse * inverse) * inverse * inverse
    near_scalar = 1.0 - 0.28125 * radial
    near_outer = 0.09375 * inverse
    nearby = radial < 2.0
    scalar = jnp.where(itself, 1.0, jnp.where(nearby, near_scalar, far_scalar))
    outer_part = jnp.where(itself, 0.0, jnp.where(nearby, near_outer, far_outer))
    return (scalar, outer_part)


def contract(left, kernel):
    return lax.dot_general(
        left,
        kernel,
        (((1,), (1,)), ((), ())),
        precision=highest,
        preferred_element_type=jnp.float32,
    )


def tile_product(row_pos, row_ids, col_pos, col_ids, vectors):
    width = vectors.shape[1]
    delta = row_pos[:, :, None] - col_pos[:, None, :]
    dist_sq = delta[0] * delta[0] + delta[1] * delta[1] + delta[2] * delta[2]
    itself = row_ids[:, None] == col_ids[None, :]
    scalar, outer_part = tile_factors(dist_sq, itself)
    result = []
    for component in range(3):
        diag_kernel = scalar + outer_part * delta[component] * delta[component]
        result.append(contract(vectors[component], diag_kernel))
    for first, second in ((0, 1), (0, 2), (1, 2)):
        cross = outer_part * delta[first] * delta[second]
        both = contract(jnp.concatenate([vectors[second], vectors[first]], axis=0), cross)
        result[first] = result[first] + both[:width]
        result[second] = result[second] + both[width:]
    return jnp.stack(result)


def blocked_product(row_pos, row_ids, col_pos, col_ids, vectors):
    rows = row_pos.shape[1]
    block = math.gcd(rows, 512)

    def row_block(index):
        begin = index * block
        pos_block = lax.dynamic_slice_in_dim(row_pos, begin, block, 1)
        id_block = lax.dynamic_slice_in_dim(row_ids, begin, block, 0)
        return tile_product(pos_block, id_block, col_pos, col_ids, vectors)

    pieces = lax.map(row_block, jnp.arange(rows // block, dtype=jnp.int32))
    return jnp.moveaxis(pieces, 0, 2).reshape(3, vectors.shape[1], rows)


def gram_of(left, right):
    return jnp.einsum("asp,atp->st", left, right, precision=highest)


def stacked_gram(stacked, right):
    return jnp.einsum("kasp,atp->kst", stacked, right, precision=highest)


def stacked_remove(stacked, weights):
    return jnp.einsum("kasp,kst->atp", stacked, weights, precision=highest)


def block_remove(member, weights):
    return jnp.einsum("asp,st->atp", member, weights, precision=highest)


def rotate(block, matrix):
    return jnp.einsum("atp,ts->asp", block, matrix, precision=highest)


def cholesky_pair(gram):
    order = gram.shape[0]
    places = jnp.arange(order, dtype=jnp.int32)
    lower = jnp.zeros((order, order), jnp.float32)
    for column in range(order):
        needed = gram[:, column] - jnp.dot(
            lower, lower[column, :], precision=highest, preferred_element_type=jnp.float32
        )
        pivot = jnp.sqrt(needed[column])
        entries = jnp.where(places >= column, needed / pivot, 0.0)
        marker = (places == column).astype(jnp.float32)
        lower = lower + entries[:, None] * marker[None, :]
    solved = jnp.zeros((order, order), jnp.float32)
    for row in range(order):
        marker = (places == row).astype(jnp.float32)
        fresh = (
            marker
            - jnp.dot(lower[row, :], solved, precision=highest, preferred_element_type=jnp.float32)
        ) / lower[row, row]
        solved = solved + marker[:, None] * fresh[None, :]
    return (lower.T, solved.T)


def tridiagonal(diagonal_blocks, lower_blocks):
    width = diagonal_blocks[0].shape[0]
    order = len(diagonal_blocks) * width
    matrix = jnp.zeros((order, order), jnp.float32)
    for index, block in enumerate(diagonal_blocks):
        offset = index * width
        matrix = matrix.at[offset : offset + width, offset : offset + width].set(block)
    for index, block in enumerate(lower_blocks):
        offset = index * width
        matrix = matrix.at[offset + width : offset + 2 * width, offset : offset + width].set(block)
        matrix = matrix.at[offset : offset + width, offset + width : offset + 2 * width].set(
            block.T
        )
    return matrix


def matrix_root(matrix):
    identity = jnp.eye(matrix.shape[0], dtype=jnp.float32)
    scale = jnp.sqrt(jnp.sum(matrix * matrix))

    def newton(turn, carry):
        current, other = carry
        factor = 1.5 * identity - 0.5 * jnp.dot(
            other, current, precision=highest, preferred_element_type=jnp.float32
        )
        return (
            jnp.dot(current, factor, precision=highest, preferred_element_type=jnp.float32),
            jnp.dot(factor, other, precision=highest, preferred_element_type=jnp.float32),
        )

    current, other = lax.fori_loop(0, ROOT_STEPS, newton, (matrix / scale, identity))
    return current * jnp.sqrt(scale)


def first_pass(basis, image):
    work = image
    single = None
    for member in basis:
        single = lax.psum(gram_of(member, work), ("wide", "narrow"))
        work = work - block_remove(member, single)
    return (single, work)


def second_pass(basis, work):
    stacked = jnp.stack(basis)
    again, raw_gram = lax.psum(
        (stacked_gram(stacked, work), gram_of(work, work)), ("wide", "narrow")
    )
    work = work - stacked_remove(stacked, again)
    gram = raw_gram - jnp.einsum("kst,ksu->tu", again, again, precision=highest)
    return (work, gram)


def per_device(positions, noise):
    width = noise.shape[1]
    local = noise.shape[2]
    narrow_count = lax.axis_size("narrow")
    row_pos = lax.all_gather(positions, "narrow", axis=1, tiled=True)
    col_pos = lax.all_gather(positions, "wide", axis=1, tiled=True)
    row_ids = lax.axis_index("wide") * (narrow_count * local) + jnp.arange(
        narrow_count * local, dtype=jnp.int32
    )
    places = jnp.arange(col_pos.shape[1], dtype=jnp.int32)
    col_ids = (
        places // local * (narrow_count * local) + lax.axis_index("narrow") * local + places % local
    )
    noise_gram = lax.psum(gram_of(noise, noise), ("wide", "narrow"))
    start_upper, start_inverse = cholesky_pair(noise_gram)
    basis = [rotate(noise, start_inverse)]
    diagonal_blocks = []
    lower_blocks = []
    for index in range(ITERS):
        empty = jnp.zeros((3, width, row_pos.shape[1]), jnp.float32)
        partial_rows = empty + blocked_product(
            row_pos,
            row_ids,
            col_pos,
            col_ids,
            lax.all_gather(basis[index], "wide", axis=2, tiled=True),
        )
        product = lax.psum_scatter(partial_rows, "narrow", scatter_dimension=2, tiled=True)
        if index + 1 == ITERS:
            current_block = lax.psum(gram_of(basis[index], product), ("wide", "narrow"))
            diagonal_blocks.append(0.5 * (current_block + current_block.T))
        else:
            current_block, work = first_pass(basis, product)
            diagonal_blocks.append(0.5 * (current_block + current_block.T))
            work, gram = second_pass(basis, work)
            upper, inverse = cholesky_pair(gram)
            lower_blocks.append(upper)
            basis.append(rotate(work, inverse))
    root = matrix_root(tridiagonal(diagonal_blocks, lower_blocks))
    mixing = jnp.dot(
        root[:, :width], start_upper, precision=highest, preferred_element_type=jnp.float32
    ).reshape(ITERS, width, width)
    return jnp.einsum("katp,kts->asp", jnp.stack(basis), mixing, precision=highest)


def solution(mesh):
    return jax.shard_map(
        per_device,
        mesh=mesh,
        in_specs=(P(None, ("wide", "narrow")), P(None, None, ("wide", "narrow"))),
        out_specs=P(None, None, ("wide", "narrow")),
        check_vma=False,
    )
```

profile of v0, /device:TPU:0, one launch (start us, length us, event | category | flops | bytes accessed | tf_op | source)
XLA Modules:
  0.0 678.2 jit_solution(14943982212568380633)
XLA Ops:
  6.5 28.2 %all_gather.17 = f32[3,1024]{1,0:T(4,128)S(1)} all-gather(f32[3,128]{1,0:T(4,128)} %param.18), channel_id=1, replica_groups=mesh['wide'=8,'narrow'=4] {'wide'}, dimensions={1}, use_global_device_ids=true | all-gather | bytes 13824 | tf_op jit(solution)/shard_map/all_gather | solution.py:169
  34.7 5.3 all_gather.16
  40.5 4.1 fusion.9
  44.6 3.1 bitcast_multiply_fusion.4
  47.8 2.9 bitcast_multiply_fusion.1
  50.9 38.9 %psum.63 = f32[16,16]{1,0:T(8,128)S(1)} all-reduce(f32[16,16]{1,0:T(8,128)S(1)} %convolution_bitcast_fusion.16), channel_id=1, replica_groups=mesh['wide'=8,'narrow'=4] {'wide','narrow'}, use_global_device_ids=true, to_apply=%region_0.1 | all-reduce | flops 256 | bytes 2048 | tf_op jit(solution)/shard_map/psum | solution.py:177
  119.2 0.9 fusion.142
  122.6 1.0 fusion.146
  125.3 0.9 fusion.149
  128.0 30.8 %all_gather.15 = f32[3,16,1024]{2,1,0:T(8,128)S(1)} all-gather(f32[3,16,128]{2,1,0:T(8,128)S(1)} %bitcast.1264), channel_id=1, replica_groups=mesh['wide'=8,'narrow'=4] {'wide'}, dimensions={2}, use_global_device_ids=true | all-gather | bytes 221184 | tf_op jit(solution)/shard_map/all_gather | solution.py:189
  158.8 3.7 fusion.190
  162.6 2.0 fusion.192
  164.6 2.0 fusion.191
  166.6 3.2 fusion.13
  169.9 1.8 fusion.24
  171.7 1.9 fusion.22
  173.6 1.8 fusion.20
  177.5 17.6 %reduce-scatter.4.cloned.1.call-done = f32[3,16,128]{2,1,0:T(8,128)} async-done(((f32[3,16,512]{2,1,0:T(8,128)}), f32[3,16,128]{2,1,0:T(8,128)}) %reduce-scatter.4.cloned.1.call-update) | async-done | bytes 24592 | tf_op jit(solution)/shard_map/reduce_scatter | solution.py:191
  196.0 39.4 %psum.64 = f32[16,16]{1,0:T(8,128)S(1)} all-reduce(f32[16,16]{1,0:T(8,128)S(1)} %convolution_bitcast_fusion.15), channel_id=1, replica_groups=mesh['wide'=8,'narrow'=4] {'wide','narrow'}, use_global_device_ids=true, to_apply=%region_2.3 | all-reduce | flops 256 | bytes 2048 | tf_op jit(solution)/shard_map/psum | solution.py:149
  235.3 1.0 fusion.41
  236.6 41.5 %all-reduce.2 = (f32[16,16]{1,0:T(8,128)S(1)}, f32[16,16]{1,0:T(8,128)S(1)}) all-reduce(f32[16,16]{1,0:T(8,128)S(1)} %convolution_bitcast_fusion.13, f32[16,16]{1,0:T(8,128)S(1)} %convolution_bitcast_fusion.14), channel_id=1, replica_groups=mesh['wide'=8,'narrow'=4] {'wide','narrow'}, use_global_device_ids=true, to_apply=%region_4.5 | all-reduce | flops 512 | bytes 4096 | tf_op jit(solution)/shard_map/psum | solution.py:156
  307.1 0.9 fusion.157
  316.6 30.6 %all_gather.18 = f32[3,16,1024]{2,1,0:T(8,128)S(1)} all-gather(f32[3,16,128]{2,1,0:T(8,128)S(1)} %bitcast.1268), channel_id=1, replica_groups=mesh['wide'=8,'narrow'=4] {'wide'}, dimensions={2}, use_global_device_ids=true | all-gather | bytes 221184 | tf_op jit(solution)/shard_map/all_gather | solution.py:189
  347.3 2.0 fusion.187
  349.3 2.0 fusion.189
  351.4 2.0 fusion.188
  353.4 1.8 fusion.30
  355.3 1.8 fusion.28
  357.1 1.9 fusion.26
  359.9 19.5 %reduce-scatter.6.cloned.1.call-done = f32[3,16,128]{2,1,0:T(8,128)} async-done(((f32[3,16,512]{2,1,0:T(8,128)}), f32[3,16,128]{2,1,0:T(8,128)}) %reduce-scatter.6.cloned.1.call-update) | async-done | bytes 24592 | tf_op jit(solution)/shard_map/reduce_scatter | solution.py:191
  380.3 39.4 %psum.67 = f32[16,16]{0,1:T(8,128)S(1)} all-reduce(f32[16,16]{0,1:T(8,128)S(1)} %convolution_bitcast_fusion.12), channel_id=1, replica_groups=mesh['wide'=8,'narrow'=4] {'wide','narrow'}, use_global_device_ids=true, to_apply=%region_6.7 | all-reduce | flops 256 | bytes 2048 | tf_op jit(solution)/shard_map/psum | solution.py:149
  419.6 0.9 fusion.39
  420.7 41.1 %psum.68 = f32[16,16]{0,1:T(8,128)S(1)} all-reduce(f32[16,16]{0,1:T(8,128)S(1)} %convolution_bitcast_fusion.11), channel_id=1, replica_groups=mesh['wide'=8,'narrow'=4] {'wide','narrow'}, use_global_device_ids=true, to_apply=%region_7.8 | all-reduce | flops 256 | bytes 2048 | tf_op jit(solution)/shard_map/psum | solution.py:149
  462.3 39.5 %all-reduce.1 = (f32[2,16,16]{2,1,0:T(8,128)S(1)}, f32[16,16]{1,0:T(8,128)S(1)}) all-reduce(f32[2,16,16]{2,1,0:T(8,128)S(1)} %convolution_bitcast_fusion.7, f32[16,16]{1,0:T(8,128)S(1)} %convolution_bitcast_fusion.10), channel_id=1, replica_groups=mesh['wide'=8,'narrow'=4] {'wide','narrow'}, use_global_device_ids=true, to_apply=%region_9.10 | all-reduce | flops 768 | bytes 6144 | tf_op jit(solution)/shard_map/psum | solution.py:156
  530.7 0.9 fusion.173
  540.3 30.8 %all_gather.19 = f32[3,16,1024]{2,1,0:T(8,128)S(1)} all-gather(f32[3,16,128]{2,1,0:T(8,128)S(1)} %bitcast.1272), channel_id=1, replica_groups=mesh['wide'=8,'narrow'=4] {'wide'}, dimensions={2}, use_global_device_ids=true | all-gather | bytes 221184 | tf_op jit(solution)/shard_map/all_gather | solution.py:189
  571.1 2.0 fusion.184
  573.1 2.0 fusion.186
  575.2 2.0 fusion.185
  577.2 1.8 fusion.36
  579.0 1.8 fusion.34
  580.9 1.9 fusion.32
  584.3 19.2 %reduce-scatter.8.cloned.1.call-done = f32[3,16,128]{2,1,0:T(8,128)} async-done(((f32[3,16,512]{2,1,0:T(8,128)}), f32[3,16,128]{2,1,0:T(8,128)}) %reduce-scatter.8.cloned.1.call-update) | async-done | bytes 24592 | tf_op jit(solution)/shard_map/reduce_scatter | solution.py:191
  604.4 39.6 %psum.71 = f32[16,16]{0,1:T(8,128)S(1)} all-reduce(f32[16,16]{0,1:T(8,128)S(1)} %convolution_bitcast_fusion.8), channel_id=1, replica_groups=mesh['wide'=8,'narrow'=4] {'wide','narrow'}, use_global_device_ids=true, to_apply=%region_11.12 | all-reduce | flops 256 | bytes 2048 | tf_op jit(solution)/shard_map/psum | solution.py:193
  645.4 1.9 dynamic-slice_select_fusion
  647.3 2.0 scatter.30
  652.4 17.9 %while.15 = (s32[]{:T(128)}, f32[48,48]{0,1:T(8,128)S(1)}, f32[48,48]{1,0:T(8,128)S(1)}, s32[]{:T(128)}) while((s32[]{:T(128)}, f32[48,48]{0,1:T(8,128)S(1)}, f32[48,48]{1,0:T(8,128)S(1)}, s32[]{:T(128)}) %tuple.168), condition=%wide.region_15.16_spmd.clone, body=%wide.region_14.15_spmd.clone.sunk | while | flops 3990530 | bytes 119861 | solution.py:141
  670.5 0.9 convolution_bitcast_fusion.1
  (491 shorter events, 107.3 us)
Async XLA Ops:
  6.5 44.2 %copy-start = (f32[3,16,128]{2,1,0:T(8,128)S(1)}, f32[3,16,128]{2,1,0:T(8,128)}, u32[]{:S(2)}) copy-start(f32[3,16,128]{2,1,0:T(8,128)} %param.19) | copy-start | bytes 73732
  6.5 188.5 %reduce-scatter.4.cloned.1.call-start = ((), (), s32[]{:S(2)}) async-start(), calls=%async_computation.3 | async-start | bytes 122880 | tf_op jit(solution)/shard_map/reduce_scatter | solution.py:191
  40.5 7.3 %copy-start.1 = (f32[3,512,1024]{2,1,0:T(8,128)}, f32[3,512,1024]{2,1,0:T(8,128)S(1)}, u32[]{:S(2)}) copy-start(f32[3,512,1024]{2,1,0:T(8,128)S(1)} %broadcast_subtract_fusion) | copy-start | bytes 18874372
  110.4 52.2 %copy-start.6 = (f32[512,1024]{1,0:T(8,128)S(1)}, f32[512,1024]{1,0:T(8,128)}, u32[]{:S(2)}) copy-start(f32[512,1024]{1,0:T(8,128)} %get-tuple-element.254) | copy-start | bytes 6291460
  122.6 42.0 %copy-start.3 = (f32[512,1024]{1,0:T(8,128)S(1)}, f32[512,1024]{1,0:T(8,128)}, u32[]{:S(2)}) copy-start(f32[512,1024]{1,0:T(8,128)} %get-tuple-element.250) | copy-start | bytes 6291460
  158.8 7.8 %copy-start.2 = (f32[3,512,1024]{2,1,0:T(8,128)S(1)}, f32[3,512,1024]{2,1,0:T(8,128)}, u32[]{:S(2)}) copy-start(f32[3,512,1024]{2,1,0:T(8,128)} %copy-done.1) | copy-start | bytes 18874372
  169.9 3.7 copy-start.11
  169.9 3.7 copy-start.14
  176.2 203.2 %reduce-scatter.6.cloned.1.call-start = ((), (), s32[]{:S(2)}) async-start(), calls=%async_computation.4 | async-start | bytes 122880 | tf_op jit(solution)/shard_map/reduce_scatter | solution.py:191
  280.8 66.5 %copy-start.9 = (f32[512,1024]{1,0:T(8,128)S(1)}, f32[512,1024]{1,0:T(8,128)}, u32[]{:S(2)}) copy-start(f32[512,1024]{1,0:T(8,128)} %get-tuple-element.255) | copy-start | bytes 6291460
  309.6 39.7 %copy-start.7 = (f32[512,1024]{1,0:T(8,128)S(1)}, f32[512,1024]{1,0:T(8,128)}, u32[]{:S(2)}) copy-start(f32[512,1024]{1,0:T(8,128)} %get-tuple-element.254) | copy-start | bytes 6291460
  347.3 4.1 copy-start.4
  349.3 4.1 copy-start.15
  351.4 3.9 copy-start.12
  359.7 243.9 %reduce-scatter.8.cloned.1.call-start = ((), (), s32[]{:S(2)}) async-start(), calls=%async_computation.5 | async-start | bytes 122880 | tf_op jit(solution)/shard_map/reduce_scatter | solution.py:191
  504.4 66.6 %copy-start.10 = (f32[512,1024]{1,0:T(8,128)S(1)}, f32[512,1024]{1,0:T(8,128)}, u32[]{:S(2)}) copy-start(f32[512,1024]{1,0:T(8,128)} %get-tuple-element.255) | copy-start | bytes 6291460
  533.2 39.9 %copy-start.8 = (f32[512,1024]{1,0:T(8,128)S(1)}, f32[512,1024]{1,0:T(8,128)}, u32[]{:S(2)}) copy-start(f32[512,1024]{1,0:T(8,128)} %get-tuple-element.254) | copy-start | bytes 6291460
  571.1 4.1 copy-start.5
  573.1 4.1 copy-start.16
  575.1 3.9 copy-start.13
Sparse Core Ops, SparseCore 0:
  176.3 18.7 reduce-scatter.3
  359.8 19.4 reduce-scatter.5
  583.5 20.0 reduce-scatter.7
where the time goes:
time: 686 us; the launch traced here: 678 us
  blocking collectives  405 us (59%)
  matrix products  107 us (16%)
  waiting for transfers between devices  56.3 us (8%)
  between operations  46.8 us (7%)
  local copies, waits for them, and re-layouts  37.3 us (5%)
  other arithmetic  24.4 us (4%)
    psum x3, blocking collectives, first_pass(): single = lax.psum(gram_of(member, work), ('wide', 'narrow'))  120 us
    all_gather x3, blocking collectives, per_device(): lax.all_gather(basis[index], 'wide', axis=2, tiled=True)  92.2 us
    psum x2, blocking collectives, second_pass(): lax.psum((stacked_gram(stacked, work), gram_of(work, work)), ('wide', 'na...  81 us
    reduce_scatter x3, waiting for transfers between devices, per_device(): lax.psum_scatter(partial_rows, 'narrow', scatter_dimension=2, tiled=True)  56.3 us
    psum x1, blocking collectives, per_device(): current_block = lax.psum(gram_of(basis[index], product), ('wide', 'narrow'))  39.6 us
    dot_general x48, matrix products, cholesky_pair(): jnp.dot(lower[row, :], solved, precision=highest, preferred_element_type=...  39.5 us
    psum x1, blocking collectives, per_device(): noise_gram = lax.psum(gram_of(noise, noise), ('wide', 'narrow'))  38.9 us
    dot_general x18, matrix products, contract(): lax.dot_general(left, kernel, (((1,), (1,)), ((), ())), precision=highest...  36.4 us
  transfers between devices with their start and end apart: 3, of which 3 were waited for; matrix products, arithmetic and copies ran while one was open for 0% of the time, Pallas kernels for 0%

commit v1 on v0

--- a/solution.py
+++ b/solution.py
@@ -146,7 +146,9 @@
     work = image
     single = None
     for member in basis:
-        single = lax.psum(gram_of(member, work), ("wide", "narrow"))
+        x = gram_of(member, work)
+        parts = lax.all_gather(x, ("wide", "narrow"), axis=0, tiled=False)
+        single = parts.sum(axis=0)
         work = work - block_remove(member, single)
     return (single, work)
 

time: 686 us -> 681 us (level)
    all_gather x0 -> x3, blocking collectives: none -> 120 us  [first_pass(): parts = lax.all_gather(x, ('wide', 'narrow'), axis=0, tiled=False)]
    psum x3 -> x0, blocking collectives: 120 us -> none  [first_pass(): single = lax.psum(gram_of(member, work), ('wide', 'narrow'))]
where the time goes in v1:
time: 681 us; the launch traced here: 673 us
  blocking collectives  399 us (59%)
  matrix products  107 us (16%)
  waiting for transfers between devices  56.7 us (8%)
  between operations  47 us (7%)
  local copies, waits for them, and re-layouts  37.3 us (5%)
  other arithmetic  24.5 us (4%)
    all_gather x3, blocking collectives, first_pass(): parts = lax.all_gather(x, ('wide', 'narrow'), axis=0, tiled=False)  120 us
    all_gather x3, blocking collectives, per_device(): lax.all_gather(basis[index], 'wide', axis=2, tiled=True)  92.5 us
    psum x2, blocking collectives, second_pass(): lax.psum((stacked_gram(stacked, work), gram_of(work, work)), ('wide', 'na...  74.6 us
    reduce_scatter x3, waiting for transfers between devices, per_device(): lax.psum_scatter(partial_rows, 'narrow', scatter_dimension=2, tiled=True)  56.6 us
    psum x1, blocking collectives, per_device(): current_block = lax.psum(gram_of(basis[index], product), ('wide', 'narrow'))  39.6 us
    dot_general x48, matrix products, cholesky_pair(): jnp.dot(lower[row, :], solved, precision=highest, preferred_element_type=...  39.5 us
    psum x1, blocking collectives, per_device(): noise_gram = lax.psum(gram_of(noise, noise), ('wide', 'narrow'))  38.9 us
    dot_general x18, matrix products, contract(): lax.dot_general(left, kernel, (((1,), (1,)), ((), ())), precision=highest...  36.4 us
  transfers between devices with their start and end apart: 3, of which 3 were waited for; matrix products, arithmetic and copies ran while one was open for 0% of the time, Pallas kernels for 0%

profile of v1, /device:TPU:0, one launch (start us, length us, event | category | flops | bytes accessed | tf_op | source)
XLA Modules:
  0.0 673.0 jit_solution(2929327929122243327)
XLA Ops:
  6.5 28.2 %all_gather.35 = f32[3,1024]{1,0:T(4,128)S(1)} all-gather(f32[3,128]{1,0:T(4,128)} %param.18), channel_id=1, replica_groups=mesh['wide'=8,'narrow'=4] {'wide'}, dimensions={1}, use_global_device_ids=true | all-gather | bytes 13824 | tf_op jit(solution)/shard_map/all_gather | solution.py:171
  34.7 5.3 all_gather.34
  40.5 4.1 fusion.9
  44.6 3.1 bitcast_multiply_fusion.4
  47.8 2.9 bitcast_multiply_fusion.1
  50.9 38.9 %psum.42 = f32[16,16]{1,0:T(8,128)S(1)} all-reduce(f32[16,16]{1,0:T(8,128)S(1)} %convolution_bitcast_fusion.16), channel_id=1, replica_groups=mesh['wide'=8,'narrow'=4] {'wide','narrow'}, use_global_device_ids=true, to_apply=%region_0.1 | all-reduce | flops 256 | bytes 2048 | tf_op jit(solution)/shard_map/psum | solution.py:179
  119.2 0.9 fusion.142
  122.6 1.0 fusion.146
  125.2 0.9 fusion.149
  128.0 31.2 %all_gather.33 = f32[3,16,1024]{2,1,0:T(8,128)S(1)} all-gather(f32[3,16,128]{2,1,0:T(8,128)S(1)} %bitcast.1267), channel_id=1, replica_groups=mesh['wide'=8,'narrow'=4] {'wide'}, dimensions={2}, use_global_device_ids=true | all-gather | bytes 221184 | tf_op jit(solution)/shard_map/all_gather | solution.py:191
  159.2 3.7 fusion.190
  162.9 2.0 fusion.192
  165.0 2.0 fusion.191
  167.0 3.2 fusion.13
  170.2 1.8 fusion.24
  172.1 1.9 fusion.22
  174.0 1.8 fusion.20
  177.8 17.6 %reduce-scatter.4.cloned.1.call-done = f32[3,16,128]{2,1,0:T(8,128)} async-done(((f32[3,16,512]{2,1,0:T(8,128)}), f32[3,16,128]{2,1,0:T(8,128)}) %reduce-scatter.4.cloned.1.call-update) | async-done | bytes 24592 | tf_op jit(solution)/shard_map/reduce_scatter | solution.py:193
  196.3 41.2 %all-gather = f32[512,16]{1,0:T(8,128)S(1)} all-gather(f32[16,16]{1,0:T(8,128)S(1)} %convolution_bitcast_fusion.15), channel_id=2, replica_groups=mesh['wide'=8,'narrow'=4] {'wide','narrow'}, dimensions={0}, use_global_device_ids=true | all-gather | bytes 33792 | tf_op jit(solution)/shard_map/all_gather | solution.py:150
  237.6 1.0 fusion.41
  238.8 37.2 %all-reduce.2 = (f32[16,16]{1,0:T(8,128)S(1)}, f32[16,16]{1,0:T(8,128)S(1)}) all-reduce(f32[16,16]{1,0:T(8,128)S(1)} %convolution_bitcast_fusion.13, f32[16,16]{1,0:T(8,128)S(1)} %convolution_bitcast_fusion.14), channel_id=1, replica_groups=mesh['wide'=8,'narrow'=4] {'wide','narrow'}, use_global_device_ids=true, to_apply=%region_4.5 | all-reduce | flops 512 | bytes 4096 | tf_op jit(solution)/shard_map/psum | solution.py:158
  305.0 0.9 fusion.157
  314.5 30.7 %all_gather.38 = f32[3,16,1024]{2,1,0:T(8,128)S(1)} all-gather(f32[3,16,128]{2,1,0:T(8,128)S(1)} %bitcast.1274), channel_id=1, replica_groups=mesh['wide'=8,'narrow'=4] {'wide'}, dimensions={2}, use_global_device_ids=true | all-gather | bytes 221184 | tf_op jit(solution)/shard_map/all_gather | solution.py:191
  345.3 2.0 fusion.187
  347.4 2.0 fusion.189
  349.4 2.0 fusion.188
  351.4 1.8 fusion.30
  353.3 1.8 fusion.28
  355.1 1.9 fusion.26
  357.9 19.3 %reduce-scatter.6.cloned.1.call-done = f32[3,16,128]{2,1,0:T(8,128)} async-done(((f32[3,16,512]{2,1,0:T(8,128)}), f32[3,16,128]{2,1,0:T(8,128)}) %reduce-scatter.6.cloned.1.call-update) | async-done | bytes 24592 | tf_op jit(solution)/shard_map/reduce_scatter | solution.py:193
  378.1 41.3 %all-gather.1 = f32[512,16]{1,0:T(8,128)S(1)} all-gather(f32[16,16]{1,0:T(8,128)S(1)} %convolution_bitcast_fusion.12), channel_id=3, replica_groups=mesh['wide'=8,'narrow'=4] {'wide','narrow'}, dimensions={0}, use_global_device_ids=true | all-gather | bytes 33792 | tf_op jit(solution)/shard_map/all_gather | solution.py:150
  419.5 1.0 fusion.39
  420.6 37.4 %all-gather.2 = f32[512,16]{1,0:T(8,128)S(1)} all-gather(f32[16,16]{1,0:T(8,128)S(1)} %convolution_bitcast_fusion.11), channel_id=4, replica_groups=mesh['wide'=8,'narrow'=4] {'wide','narrow'}, dimensions={0}, use_global_device_ids=true | all-gather | bytes 33792 | tf_op jit(solution)/shard_map/all_gather | solution.py:150
  458.6 37.4 %all-reduce.1 = (f32[2,16,16]{2,1,0:T(8,128)S(1)}, f32[16,16]{1,0:T(8,128)S(1)}) all-reduce(f32[2,16,16]{2,1,0:T(8,128)S(1)} %convolution_bitcast_fusion.7, f32[16,16]{1,0:T(8,128)S(1)} %convolution_bitcast_fusion.10), channel_id=1, replica_groups=mesh['wide'=8,'narrow'=4] {'wide','narrow'}, use_global_device_ids=true, to_apply=%region_9.10 | all-reduce | flops 768 | bytes 6144 | tf_op jit(solution)/shard_map/psum | solution.py:158
  524.9 0.9 fusion.173
  534.5 30.6 %all_gather.43 = f32[3,16,1024]{2,1,0:T(8,128)S(1)} all-gather(f32[3,16,128]{2,1,0:T(8,128)S(1)} %bitcast.1278), channel_id=1, replica_groups=mesh['wide'=8,'narrow'=4] {'wide'}, dimensions={2}, use_global_device_ids=true | all-gather | bytes 221184 | tf_op jit(solution)/shard_map/all_gather | solution.py:191
  565.1 2.0 fusion.184
  567.2 2.0 fusion.186
  569.2 2.0 fusion.185
  571.2 1.8 fusion.36
  573.1 1.8 fusion.34
  574.9 1.9 fusion.32
  578.4 19.7 %reduce-scatter.8.cloned.1.call-done = f32[3,16,128]{2,1,0:T(8,128)} async-done(((f32[3,16,512]{2,1,0:T(8,128)}), f32[3,16,128]{2,1,0:T(8,128)}) %reduce-scatter.8.cloned.1.call-update) | async-done | bytes 24592 | tf_op jit(solution)/shard_map/reduce_scatter | solution.py:193
  599.0 39.6 %psum.47 = f32[16,16]{1,0:T(8,128)S(1)} all-reduce(f32[16,16]{1,0:T(8,128)S(1)} %convolution_bitcast_fusion.8), channel_id=1, replica_groups=mesh['wide'=8,'narrow'=4] {'wide','narrow'}, use_global_device_ids=true, to_apply=%region_11.12 | all-reduce | flops 256 | bytes 2048 | tf_op jit(solution)/shard_map/psum | solution.py:195
  639.9 1.9 dynamic-slice_select_fusion
  641.9 2.0 scatter.30
  646.9 17.9 %while.15 = (s32[]{:T(128)}, f32[48,48]{0,1:T(8,128)S(1)}, f32[48,48]{1,0:T(8,128)S(1)}, s32[]{:T(128)}) while((s32[]{:T(128)}, f32[48,48]{0,1:T(8,128)S(1)}, f32[48,48]{1,0:T(8,128)S(1)}, s32[]{:T(128)}) %tuple.169), condition=%wide.region_15.16_spmd.clone, body=%wide.region_14.15_spmd.clone.sunk | while | flops 3990530 | bytes 119861 | solution.py:141
  665.1 0.9 convolution_bitcast_fusion.1
  (494 shorter events, 107.5 us)
Async XLA Ops:
  6.5 44.2 %copy-start = (f32[3,16,128]{2,1,0:T(8,128)S(1)}, f32[3,16,128]{2,1,0:T(8,128)}, u32[]{:S(2)}) copy-start(f32[3,16,128]{2,1,0:T(8,128)} %param.19) | copy-start | bytes 73732
  6.5 188.9 %reduce-scatter.4.cloned.1.call-start = ((), (), s32[]{:S(2)}) async-start(), calls=%async_computation.3 | async-start | bytes 122880 | tf_op jit(solution)/shard_map/reduce_scatter | solution.py:193
  40.5 7.3 %copy-start.1 = (f32[3,512,1024]{2,1,0:T(8,128)}, f32[3,512,1024]{2,1,0:T(8,128)S(1)}, u32[]{:S(2)}) copy-start(f32[3,512,1024]{2,1,0:T(8,128)S(1)} %broadcast_subtract_fusion) | copy-start | bytes 18874372
  110.4 52.5 %copy-start.6 = (f32[512,1024]{1,0:T(8,128)S(1)}, f32[512,1024]{1,0:T(8,128)}, u32[]{:S(2)}) copy-start(f32[512,1024]{1,0:T(8,128)} %get-tuple-element.257) | copy-start | bytes 6291460
  122.6 42.4 %copy-start.3 = (f32[512,1024]{1,0:T(8,128)S(1)}, f32[512,1024]{1,0:T(8,128)}, u32[]{:S(2)}) copy-start(f32[512,1024]{1,0:T(8,128)} %get-tuple-element.253) | copy-start | bytes 6291460
  159.2 7.8 %copy-start.2 = (f32[3,512,1024]{2,1,0:T(8,128)S(1)}, f32[3,512,1024]{2,1,0:T(8,128)}, u32[]{:S(2)}) copy-start(f32[3,512,1024]{2,1,0:T(8,128)} %copy-done.1) | copy-start | bytes 18874372
  170.2 3.7 copy-start.11
  170.2 3.7 copy-start.14
  176.5 200.7 %reduce-scatter.6.cloned.1.call-start = ((), (), s32[]{:S(2)}) async-start(), calls=%async_computation.4 | async-start | bytes 122880 | tf_op jit(solution)/shard_map/reduce_scatter | solution.py:193
  278.7 66.6 %copy-start.9 = (f32[512,1024]{1,0:T(8,128)S(1)}, f32[512,1024]{1,0:T(8,128)}, u32[]{:S(2)}) copy-start(f32[512,1024]{1,0:T(8,128)} %get-tuple-element.258) | copy-start | bytes 6291460
  307.5 39.8 %copy-start.7 = (f32[512,1024]{1,0:T(8,128)S(1)}, f32[512,1024]{1,0:T(8,128)}, u32[]{:S(2)}) copy-start(f32[512,1024]{1,0:T(8,128)} %get-tuple-element.257) | copy-start | bytes 6291460
  345.3 4.1 copy-start.4
  347.3 4.1 copy-start.15
  349.4 3.9 copy-start.12
  357.7 240.4 %reduce-scatter.8.cloned.1.call-start = ((), (), s32[]{:S(2)}) async-start(), calls=%async_computation.5 | async-start | bytes 122880 | tf_op jit(solution)/shard_map/reduce_scatter | solution.py:193
  498.6 66.5 %copy-start.10 = (f32[512,1024]{1,0:T(8,128)S(1)}, f32[512,1024]{1,0:T(8,128)}, u32[]{:S(2)}) copy-start(f32[512,1024]{1,0:T(8,128)} %get-tuple-element.258) | copy-start | bytes 6291460
  527.4 39.7 %copy-start.8 = (f32[512,1024]{1,0:T(8,128)S(1)}, f32[512,1024]{1,0:T(8,128)}, u32[]{:S(2)}) copy-start(f32[512,1024]{1,0:T(8,128)} %get-tuple-element.257) | copy-start | bytes 6291460
  565.1 4.1 copy-start.5
  567.2 4.1 copy-start.16
  569.2 3.9 copy-start.13
Sparse Core Ops, SparseCore 0:
  176.6 18.7 reduce-scatter.3
  357.8 19.3 reduce-scatter.5
  577.6 20.4 reduce-scatter.7
